TPU v7x, 128 devices: a whole 4x4x4 slice. The times are simulated.
128 devices in a mesh: blk: 64 (over x_lo, y, z, core), tensor: 2 (over x_hi).
Axes of the slice: x: 4 (x_hi: 2, x_lo: 2; x = x_hi * 2 + x_lo), y: 4, z: 4, core: 2. Of those that a mesh axis runs over, the one named last changes fastest.
Arguments:
- tokens: bfloat16 [256, 8192], P('blk'), may hold values from -6 to 6
- gate_weight: bfloat16 [29568, 8192], P(('blk', 'tensor')), may hold values from -0.0625 to 0.0625
- up_weight: bfloat16 [29568, 8192], P(('blk', 'tensor')), may hold values from -0.0625 to 0.0625
- down_weight: bfloat16 [29568, 8192], P(('blk', 'tensor')), may hold values from -0.03125 to 0.03125
Outputs:
- mixed: bfloat16 [256, 8192], P(('blk', 'tensor'))
All inputs are finite; a program needn't handle non-finite values.
Results may differ from a plain program's by a relative error of at most 0.009.
Values may be sent and summed in bfloat16 or wider, within the bound.
A program may use at most 64 MiB of HBM per device.

v0:
```python
import jax
import jax.numpy as jnp
from jax import lax
from jax.sharding import PartitionSpec as P


def project_rows(left, weight):
    return lax.dot_general(
        left, weight, (((1,), (1,)), ((), ())), preferred_element_type=jnp.float32
    )


def per_device(tokens, gate_weight, up_weight, down_weight):
    piece = lax.all_gather(tokens, "blk", axis=0, tiled=True)
    gate = project_rows(piece, gate_weight)
    up_part = project_rows(piece, up_weight)
    hidden = (jax.nn.silu(gate) * up_part).astype(jnp.bfloat16)
    total = lax.psum_scatter(
        jnp.dot(hidden, down_weight, preferred_element_type=jnp.float32),
        ("blk", "tensor"),
        scatter_dimension=0,
        tiled=True,
    )
    return total.astype(jnp.bfloat16)


def solution(mesh):
    placed = (
        P("blk", None),
        P(("blk", "tensor"), None),
        P(("blk", "tensor"), None),
        P(("blk", "tensor"), None),
    )
    return jax.shard_map(
        per_device,
        mesh=mesh,
        in_specs=placed,
        out_specs=P(("blk", "tensor"), None),
        check_vma=False,
    )
```

profile of v0, /device:TPU:1, one launch (start us, length us, event | category | flops | bytes accessed | tf_op | source)
XLA Modules:
  0.0 259.6 jit_solution(18180911876720562141)
XLA Ops:
  6.5 0.0 all-gather.3.cloned.1.call-start
  6.5 0.7 all-gather.3.cloned.1.call-update
  7.3 110.8 %all-gather.3.cloned.1.call-done = bf16[64,4,8192]{2,1,0:T(4,128)(2,1)} async-done(((bf16[1,4,8192]{2,1,0:T(4,128)(2,1)}), bf16[64,4,8192]{2,1,0:T(4,128)(2,1)}) %all-gather.3.cloned.1.call-update) | async-done | bytes 4194320 | tf_op jit(solution)/shard_map/all_gather | solution.py:14
  118.0 6.9 %reshape.1 = bf16[256,8192]{1,0:T(8,128)(2,1)} reshape(bf16[64,4,8192]{2,1,0:T(4,128)(2,1)} %all-gather.3.cloned.1.call-done) | data formatting | bytes 8388608
  125.0 4.7 %fusion.9 = f32[256,231]{0,1:T(8,128)S(1)} fusion(bf16[256,8192]{1,0:T(8,128)(2,1)} %reshape.1, bf16[231,8192]{1,0:T(8,128)(2,1)} %param.5), kind=kOutput, calls=%fused_computation.11 | convolution fusion | flops 968884224 | bytes 8215552 | tf_op jit(solution)/shard_map/dot_general | solution.py:8
  129.7 12.3 %fusion.1 = f32[256,8192]{1,0:T(8,128)} fusion(bf16[231,8192]{1,0:T(8,128)(2,1)} %param.7, bf16[256,8192]{1,0:T(8,128)(2,1)} %reshape.1, bf16[231,8192]{1,0:T(8,128)(2,1)} %param.6, f32[256,231]{0,1:T(8,128)S(1)} %fusion.9), kind=kOutput, calls=%fused_computation.2 | convolution fusion | flops 1938123264 | bytes 20388864 | tf_op jit(solution)/shard_map/dot_general | solution.py:19
  142.0 109.2 %all-reduce.2 = bf16[256,8192]{1,0:T(8,128)(2,1)} all-reduce(f32[256,8192]{1,0:T(8,128)} %fusion.1), channel_id=2, replica_groups=mesh['blk'=64,'tensor'=2] {'blk','tensor'}, use_global_device_ids=true, to_apply=%region_0.1.clone | all-reduce | flops 2097152 | bytes 12582912
  251.2 1.6 dynamic-slice_convert_fusion
Async XLA Ops:
  6.5 111.5 %all-gather.3.cloned.1.call-start = ((), (), s32[]{:S(2)}) async-start(), calls=%async_computation | async-start | bytes 4259840 | tf_op jit(solution)/shard_map/all_gather | solution.py:14
Sparse Core Ops, SparseCore 0:
  9.0 108.9 all-gather.2
where the time goes:
time: 262 us; the launch traced here: 260 us
  waiting for transfers between devices  111 us (42%)
  blocking collectives  109 us (42%)
  matrix products  17.1 us (7%)
  between operations  13.4 us (5%)
  local copies, waits for them, and re-layouts  8.48 us (3%)
    all_gather x1, waiting for transfers between devices, per_device(): piece = lax.all_gather(tokens, 'blk', axis=0, tiled=True)  111 us
    unnamed x1, blocking collectives  109 us
    dot_general x1, matrix products, per_device(): jnp.dot(hidden, down_weight, preferred_element_type=jnp.float32)  12.3 us
    unnamed x1, local copies, waits for them, and re-layouts  6.92 us
  transfers between devices with their start and end apart: 1, of which 1 were waited for; matrix products, arithmetic and copies ran while one was open for 0% of the time, Pallas kernels for 0%

commit v1 on v0

v1 whole, which is shorter than its diff:
```python
import jax
import jax.numpy as jnp
from jax import lax
from jax.experimental import pallas as pl
from jax.experimental.pallas import tpu as pltpu
from jax.sharding import PartitionSpec as P

F32 = jnp.float32
BF16 = jnp.bfloat16
MESH = pl.DeviceIdType.MESH
D = 8192
HALF = D // 2
TOKENS = 256

CHUNK_TILES = ((8, 7, 7), (7, 7, 7), (7, 7, 7))
ORDERS = ("xyz", "yzx", "zxy")


def chunks_of():
    chunks, start = [[], [], []], 0
    for colour, tiles in enumerate(CHUNK_TILES):
        for tile in tiles:
            chunks[colour].append((colour, start * 128, tile * 128, (tile + 1) // 2 * 128))
            start += tile
    return [chunks[colour][at] for at in range(3) for colour in range(3)]


CHUNKS = chunks_of()
NC = len(CHUNKS)
N_GATHER = 96
N_RS = 13 * NC


def kernel(
    tokens_hbm, gate_hbm, up_hbm, down_hbm, out_ref,
    own4, recv4, tok, gate_w, up_w, down_w, own, d2d_send, d2d_recv,
    sa, rl, rp, rm, sb, rb, sc, rc,
    local_sem, g_send, g_recv, r_send, r_recv,
):
    blk = lax.axis_index("blk")
    x_hi = lax.axis_index("tensor")
    core = blk % 2
    z = (blk // 2) % 4
    y = (blk // 8) % 4
    x_lo = blk // 32
    x = x_hi * 2 + x_lo
    at = {"x": x, "y": y, "z": z}

    def device(dx=0, dy=0, dz=0, dcore=0):
        tx, ty, tz = (x + dx + 4) % 4, (y + dy + 4) % 4, (z + dz + 4) % 4
        tc = (core + dcore) % 2
        return {"blk": (((tx % 2) * 4 + ty) * 4 + tz) * 2 + tc, "tensor": tx // 2}

    def shifted(axis, delta):
        return device(**{"d" + axis: delta})

    partner = device(dcore=1)

    load_tokens = pltpu.make_async_copy(tokens_hbm, own4, local_sem.at[0])
    load_tokens.start()
    loads = [
        pltpu.make_async_copy(src, dst, local_sem.at[1 + i])
        for i, (src, dst) in enumerate(((gate_hbm, gate_w), (up_hbm, up_w), (down_hbm, down_w)))
    ]
    for load in loads:
        load.start()

    barrier = pltpu.get_barrier_semaphore()
    peers = [partner] + [shifted(axis, delta) for axis in "xyz" for delta in (1, 2, 3)]
    for peer in peers:
        pl.semaphore_signal(barrier, inc=1, device_id=peer, device_id_type=MESH)
    pl.semaphore_wait(barrier, len(peers))

    sends = []
    counter = [0]

    def new_sem():
        counter[0] += 1
        return counter[0] - 1

    def send(src, dst, sem, to, pool=None):
        s, r = pool or (g_send, g_recv)
        copy = pltpu.make_async_remote_copy(
            src_ref=src, dst_ref=dst, send_sem=s.at[sem], recv_sem=r.at[sem],
            device_id=to, device_id_type=MESH,
        )
        copy.start()
        sends.append(copy)

    def arrived(ref, sem, pool=None):
        s, r = pool or (g_send, g_recv)
        pltpu.make_async_remote_copy(
            src_ref=ref, dst_ref=ref, send_sem=s.at[sem], recv_sem=r.at[sem],
            device_id=partner, device_id_type=MESH,
        ).wait_recv()

    load_tokens.wait()
    mine = pl.multiple_of(core * HALF, HALF)
    theirs = pl.multiple_of((1 - core) * HALF, HALF)
    sem = new_sem()
    send(own4.at[:, pl.ds(theirs, HALF)], recv4, sem, partner)
    arrived(recv4, sem)
    a = own4[:, pl.ds(mine, HALF)].astype(F32)
    b = recv4[...].astype(F32)
    first = core == 0
    unit = jnp.concatenate([jnp.where(first, a, b), jnp.where(first, b, a)], axis=0)
    tok[x_lo, y, z, :, pl.ds(mine, HALF)] = unit.astype(BF16)

    Q = HALF // 4
    H = Q // 2

    def cols(colour, part=None, base=None):
        base = mine if base is None else base
        if part is None:
            return pl.ds(pl.multiple_of(base + colour * Q, 128), Q)
        return pl.ds(pl.multiple_of(base + colour * Q + part * H, 128), H)

    def piece(xl, yy, zz, c):
        return tok.at[xl, yy, zz, :, c]

    everything = slice(None)
    other = 1 - x_lo

    def line(colour, first_axis, fixed, c, xl):
        if first_axis == "y":
            return tok.at[xl, :, fixed, :, c]
        return tok.at[xl, fixed, :, :, c]

    d2d_sems = []

    def forward(make_ref):
        sem = new_sem()
        ref = make_ref(mine)
        send(ref, ref, sem, partner)
        d2d_sems.append((sem, make_ref))

    axes = {0: ("y", "z"), 1: ("z", "y"), 2: ("z", "y"), 3: ("y", "z")}

    s1 = {}
    for colour in range(4):
        p, q = axes[colour]
        for delta in (1, 3, 2):
            s1[colour, delta] = new_sem()
            ref = piece(x_lo, y, z, cols(colour))
            send(ref, ref, s1[colour, delta], shifted(p, delta))

    xs, qs, ring = {}, {}, {}

    def both_x(colour, fixed, key):
        p, q = axes[colour]
        for part, delta in ((0, 1), (1, 3)):
            xs[colour, key, part] = new_sem()
            ref = line(colour, p, fixed, cols(colour, part), x_lo)
            send(ref, ref, xs[colour, key, part], shifted("x", delta))

    def start_ring(colour, xl, key):
        p, q = axes[colour]
        for delta in (1, 3):
            ring[colour, key, delta] = new_sem()
            ref = line(colour, p, at[q], cols(colour), xl)
            send(ref, ref, ring[colour, key, delta], shifted(q, delta))

    def pass_ring(colour, xl, key, delta):
        p, q = axes[colour]
        place = (at[q] - delta + 4) % 4
        ref = line(colour, p, place, cols(colour), xl)
        arrived(ref, ring[colour, key, delta])
        part = 0 if delta == 1 else 1
        ring[colour, key, delta, "far"] = new_sem()
        ref = line(colour, p, place, cols(colour, part), xl)
        send(ref, ref, ring[colour, key, delta, "far"], shifted(q, delta))
        return place

    def end_ring(colour, xl, key, delta):
        p, q = axes[colour]
        place = (at[q] + 2) % 4
        part = 0 if delta == 1 else 1
        arrived(line(colour, p, place, cols(colour, part), xl), ring[colour, key, delta, "far"])
        return place

    def forward_line(colour, fixed, xl):
        p, _ = axes[colour]
        forward(lambda base: line(colour, p, fixed, cols(colour, None, base), xl))

    for colour in range(4):
        p, q = axes[colour]
        for delta in (1, 3, 2):
            place = {p: (at[p] - delta + 4) % 4, q: at[q]}
            arrived(piece(x_lo, place["y"], place["z"], cols(colour)), s1[colour, delta])
        if colour < 2:
            start_ring(colour, x_lo, "own")
            both_x(colour, at[q], 0)
        else:
            both_x(colour, at[q], 0)
            start_ring(colour, x_lo, "own")
        forward_line(colour, at[q], x_lo)

    for colour in (0, 1):
        for delta in (1, 3):
            place = pass_ring(colour, x_lo, "own", delta)
            both_x(colour, place, delta)
            forward_line(colour, place, x_lo)
    for colour in (2, 3):
        p, q = axes[colour]
        for part in (0, 1):
            arrived(line(colour, p, at[q], cols(colour, part), other), xs[colour, 0, part])
        start_ring(colour, other, "other")
        forward_line(colour, at[q], other)
    for colour in (2, 3):
        for delta in (1, 3):
            place = pass_ring(colour, x_lo, "own", delta)
            forward_line(colour, place, x_lo)

    for colour in (0, 1):
        p, q = axes[colour]
        place = (at[q] + 2) % 4
        for delta, part, step in ((1, 0, 1), (3, 1, 3)):
            end_ring(colour, x_lo, "own", delta)
            xs[colour, 2, part] = new_sem()
            ref = line(colour, p, place, cols(colour, part), x_lo)
            send(ref, ref, xs[colour, 2, part], shifted("x", step))
        forward_line(colour, place, x_lo)
        for key in (0, 1, 3):
            place = (at[q] - key + 4) % 4
            for part in (0, 1):
                arrived(line(colour, p, place, cols(colour, part), other), xs[colour, key, part])
            forward_line(colour, place, other)
    for colour in (2, 3):
        for delta in (1, 3):
            place = pass_ring(colour, other, "other", delta)
            forward_line(colour, place, other)
    for colour in (2, 3):
        for delta in (1, 3):
            place = end_ring(colour, x_lo, "own", delta)
        forward_line(colour, place, x_lo)

    for colour in (0, 1):
        p, q = axes[colour]
        place = (at[q] + 2) % 4
        for part in (0, 1):
            arrived(line(colour, p, place, cols(colour, part), other), xs[colour, 2, part])
        forward_line(colour, place, other)
    for colour in (2, 3):
        for delta in (1, 3):
            place = end_ring(colour, other, "other", delta)
        forward_line(colour, place, other)

    for load in loads[:2]:
        load.wait()
    flat = tok.reshape(TOKENS, D)

    def project(weight, base):
        return lax.dot_general(
            flat[:, pl.ds(base, HALF)], weight[:, pl.ds(base, HALF)],
            (((1,), (1,)), ((), ())), preferred_element_type=F32,
        )

    gate = project(gate_w, mine)
    up = project(up_w, mine)
    for sem, make_ref in d2d_sems:
        arrived(make_ref(theirs), sem)
    gate = gate + project(gate_w, theirs)
    up = up + project(up_w, theirs)
    hidden = (gate / (1.0 + jnp.exp(-gate)) * up).astype(BF16)

    rho = lax.broadcasted_iota(jnp.int32, (TOKENS, TOKENS), 0)
    token = lax.broadcasted_iota(jnp.int32, (TOKENS, TOKENS), 1)
    t_core = (rho // 128 + core) % 2
    hiddens = []
    for order in ORDERS:
        where = {}
        for axis, width in zip(order, (32, 8, 2)):
            where[axis] = ((rho // width) % 4 + at[axis]) % 4
        t_blk = (((where["x"] % 2) * 4 + where["y"]) * 4 + where["z"]) * 2 + t_core
        t_row = t_blk * 4 + (where["x"] // 2) * 2 + rho % 2
        pick = jnp.where(t_row == token, 1.0, 0.0).astype(BF16)
        hiddens.append(jnp.dot(pick, hidden, preferred_element_type=F32).astype(BF16))

    pool = (r_send, r_recv)
    loads[2].wait()
    for i, (colour, start, width, left) in enumerate(CHUNKS):
        c = pl.ds(start, width)
        part = jnp.dot(hiddens[colour], down_w[:, c], preferred_element_type=F32)
        d2d_send[:, c] = part[128:].astype(BF16)
        own[:, c] = part[:128]
        send(d2d_send.at[:, c], d2d_recv.at[:, c], i * 13, partner, pool)

    for i, (colour, start, width, left) in enumerate(CHUNKS):
        axis = ORDERS[colour][0]
        c, cl, cr = pl.ds(start, width), pl.ds(start, left), pl.ds(start + left, width - left)
        arrived(d2d_recv.at[:, c], i * 13, pool)
        sa[64:96, c] = (own[64:96, c] + d2d_recv[64:96, c].astype(F32)).astype(BF16)
        send(sa.at[64:96, cl], rl.at[:, cl], i * 13 + 1, shifted(axis, 1), pool)
        send(sa.at[64:96, cr], rl.at[:, cr], i * 13 + 2, shifted(axis, 3), pool)
        sa[32:64, cr] = (own[32:64, cr] + d2d_recv[32:64, cr].astype(F32)).astype(BF16)
        send(sa.at[32:64, cr], rp.at[:, cr], i * 13 + 3, shifted(axis, 1), pool)
        sa[96:128, cl] = (own[96:128, cl] + d2d_recv[96:128, cl].astype(F32)).astype(BF16)
        send(sa.at[96:128, cl], rm.at[:, cl], i * 13 + 4, shifted(axis, 3), pool)
    for i, (colour, start, width, left) in enumerate(CHUNKS):
        axis = ORDERS[colour][0]
        c, cl, cr = pl.ds(start, width), pl.ds(start, left), pl.ds(start + left, width - left)
        arrived(rl.at[:, cl], i * 13 + 1, pool)
        sa[32:64, cl] = (
            own[32:64, cl] + d2d_recv[32:64, cl].astype(F32) + rl[:, cl].astype(F32)
        ).astype(BF16)
        send(sa.at[32:64, cl], rp.at[:, cl], i * 13 + 5, shifted(axis, 1), pool)
        arrived(rl.at[:, cr], i * 13 + 2, pool)
        sa[96:128, cr] = (
            own[96:128, cr] + d2d_recv[96:128, cr].astype(F32) + rl[:, cr].astype(F32)
        ).astype(BF16)
        send(sa.at[96:128, cr], rm.at[:, cr], i * 13 + 6, shifted(axis, 3), pool)

    for i, (colour, start, width, left) in enumerate(CHUNKS):
        axis = ORDERS[colour][1]
        c, cl, cr = pl.ds(start, width), pl.ds(start, left), pl.ds(start + left, width - left)
        arrived(rp.at[:, cr], i * 13 + 3, pool)
        arrived(rm.at[:, cl], i * 13 + 4, pool)
        arrived(rp.at[:, cl], i * 13 + 5, pool)
        arrived(rm.at[:, cr], i * 13 + 6, pool)
        total = (
            own[0:32, c] + d2d_recv[0:32, c].astype(F32)
            + rp[:, c].astype(F32) + rm[:, c].astype(F32)
        )
        own[0:8, c] = total[0:8]
        for delta in (2, 1, 3):
            sb[delta, :, c] = total[delta * 8:delta * 8 + 8].astype(BF16)
            send(sb.at[delta, :, c], rb.at[delta, :, c], i * 13 + 6 + delta, shifted(axis, delta), pool)

    for i, (colour, start, width, left) in enumerate(CHUNKS):
        axis = ORDERS[colour][2]
        c = pl.ds(start, width)
        total = own[0:8, c]
        for delta in (1, 3, 2):
            arrived(rb.at[delta, :, c], i * 13 + 6 + delta, pool)
            total = total + rb[delta, :, c].astype(F32)
        own[0:8, c] = total
        for delta in (2, 1, 3):
            sc[delta, :, c] = total[delta * 2:delta * 2 + 2].astype(BF16)
            send(sc.at[delta, :, c], rc.at[delta, :, c], i * 13 + 9 + delta, shifted(axis, delta), pool)
    for i, (colour, start, width, left) in enumerate(CHUNKS):
        c = pl.ds(start, width)
        total = own[0:2, c]
        for delta in (1, 3, 2):
            arrived(rc.at[delta, :, c], i * 13 + 9 + delta, pool)
            total = total + rc[delta, :, c].astype(F32)
        out_ref[:, c] = total.astype(BF16)

    for copy in sends:
        copy.wait_send()
    assert counter[0] <= N_GATHER


def per_device(tokens, gate_weight, up_weight, down_weight):
    hidden = gate_weight.shape[0]
    return pl.pallas_call(
        kernel,
        out_shape=jax.ShapeDtypeStruct((2, D), BF16),
        in_specs=[pl.BlockSpec(memory_space=pl.ANY)] * 4,
        out_specs=pl.BlockSpec(memory_space=pltpu.VMEM),
        scratch_shapes=[
            pltpu.VMEM((4, D), BF16),
            pltpu.VMEM((4, HALF), BF16),
            pltpu.VMEM((2, 4, 4, 8, D), BF16),
            pltpu.VMEM((hidden, D), BF16),
            pltpu.VMEM((hidden, D), BF16),
            pltpu.VMEM((hidden, D), BF16),
            pltpu.VMEM((128, D), F32),
            pltpu.VMEM((128, D), BF16),
            pltpu.VMEM((128, D), BF16),
            pltpu.VMEM((128, D), BF16),
            pltpu.VMEM((32, D), BF16),
            pltpu.VMEM((32, D), BF16),
            pltpu.VMEM((32, D), BF16),
            pltpu.VMEM((4, 8, D), BF16),
            pltpu.VMEM((4, 8, D), BF16),
            pltpu.VMEM((4, 2, D), BF16),
            pltpu.VMEM((4, 2, D), BF16),
            pltpu.SemaphoreType.DMA((4,)),
            pltpu.SemaphoreType.DMA((N_GATHER,)),
            pltpu.SemaphoreType.DMA((N_GATHER,)),
            pltpu.SemaphoreType.DMA((N_RS,)),
            pltpu.SemaphoreType.DMA((N_RS,)),
        ],
        compiler_params=pltpu.CompilerParams(
            collective_id=0, has_side_effects=True, vmem_limit_bytes=63 * 1024 * 1024
        ),
    )(tokens, gate_weight, up_weight, down_weight)


def solution(mesh):
    placed = (
        P("blk", None),
        P(("blk", "tensor"), None),
        P(("blk", "tensor"), None),
        P(("blk", "tensor"), None),
    )
    return jax.shard_map(
        per_device,
        mesh=mesh,
        in_specs=placed,
        out_specs=P(("blk", "tensor"), None),
        check_vma=False,
    )
```

time: 262 us -> 54.8 us (0.21)
  waiting for transfers between devices: 111 us -> 0 us
  blocking collectives: 109 us -> 0 us
  Pallas kernels: 0 us -> 52.6 us
  matrix products: 17.1 us -> 0 us
  between operations: 13.4 us -> 0.01 us
  local copies, waits for them, and re-layouts: 8.48 us -> 1.4 us
    all_gather x1 -> x0, waiting for transfers between devices: 111 us -> none  [per_device(): piece = lax.all_gather(tokens, 'blk', axis=0, tiled=True)]
    unnamed x1 -> x0, blocking collectives: 109 us -> none
    pallas_call x0 -> x1, Pallas kernels: none -> 52.6 us  [per_device(): pl.pallas_call(kernel, out_shape=jax.ShapeDtypeStruct((2, D), BF16), in_s...]
    dot_general x2 -> x0, matrix products: 17.1 us -> none  [the longest x1 12.3 us: per_device(): jnp.dot(hidden, down_weight, preferred_element_type=jnp.float32)]
    unnamed x1, local copies, waits for them, and re-layouts: 6.92 us -> 1.4 us
  transfers between devices with their start and end apart: 1 -> 0, of which waited for: 1 -> 0; matrix products, arithmetic and copies ran while one was open for 0% -> 0% of each run, Pallas kernels for 0% -> 0%
where the time goes in v1:
time: 54.8 us; the launch traced here: 54 us
  Pallas kernels  52.6 us (96%)
  local copies, waits for them, and re-layouts  1.4 us (3%)
    pallas_call x1, Pallas kernels, per_device(): pl.pallas_call(kernel, out_shape=jax.ShapeDtypeStruct((2, D), BF16), in_s...  52.6 us
    unnamed x1, local copies, waits for them, and re-layouts  1.4 us

profile of v1, /device:TPU:1, one launch (start us, length us, event | category | flops | bytes accessed | tf_op | source)
XLA Modules:
  0.0 54.0 jit_solution(689113956650377832)
XLA Ops:
  0.0 52.6 %shard_map.46 = bf16[2,8192]{1,0:T(2,128)(2,1)} custom-call(bf16[4,8192]{1,0:T(4,128)(2,1)} %tokens_hbm.1, bf16[231,8192]{1,0:T(8,128)(2,1)} %gate_hbm.1, bf16[231,8192]{1,0:T(8,128)(2,1)} %up_hbm.1, bf16[231,8192]{1,0:T(8,128)(2,1)} %down_hbm.1), custom_call_target="tpu_custom_call" | custom-call | tf_op jit(solution)/shard_map/pallas_call | solution.py:355
  52.6 1.4 %copy.6 = bf16[2,8192]{1,0:T(2,128)(2,1)} copy(bf16[2,8192]{1,0:T(2,128)(2,1)} %shard_map.46) | data formatting | bytes 65536
